TPU v7x, 32 devices: a whole 2x2x4 slice. The times are simulated.
32 devices in a mesh: zero: 4 (over z), width: 4 (over y, x), unit: 2 (over core).
Axes of the slice: x: 2, y: 2, z: 4, core: 2. Of those that a mesh axis runs over, the one named last changes fastest.
Arguments:
- grad_stack: float32 [64, 128, 2048], P('unit', 'zero', 'width'), parts along dimension 0, may hold values from -6 to 6
- moment_stack: float32 [64, 128, 2048], P('unit', 'zero', 'width'), parts along dimension 0, may hold values from -6 to 6
- weight_stack: float32 [64, 128, 2048], P('unit', 'zero', 'width'), parts along dimension 0, may hold values from -0.1875 to 0.1875
Outputs:
- new_weights: float32 [64, 128, 2048], P('unit', 'zero', 'width'), parts along dimension 0
- new_momentum: float32 [64, 128, 2048], P('unit', 'zero', 'width'), parts along dimension 0
There are 2 independent parts, one for each index of `unit`. A program takes and returns all parts, laid end to end along the dimension named above; each array names one. Nothing has to cross between parts.
All inputs are finite; a program needn't handle non-finite values.
Results may differ from a plain program's by a relative error of at most 0.0001.
Values sent between devices are 32-bit elements; how exact they have to be, the bound alone decides.
A program may use at most 64 MiB of HBM per device.

v0:
```python
import functools

import jax
import jax.numpy as jnp
from jax import lax
from jax.experimental import pallas as pl
from jax.experimental.pallas import tpu as pltpu
from jax.sharding import PartitionSpec as P

ITERS = 3
GATHER_FROM = 1
RESULT_FROM = 1
CHUNKS = (4, 2, 1)
MESH = pl.DeviceIdType.MESH


hold_rate = 0.95
learn_rate = 0.8
decay_rate = 0.1
keep_rate = 1.0 - learn_rate * decay_rate


def split(value):
    high = value.astype(jnp.bfloat16)
    low = (value - high.astype(jnp.float32)).astype(jnp.bfloat16)
    return high, low


def product(left, right, over):
    dims = (((1,), (over,)), ((), ()))
    dot = functools.partial(lax.dot_general, dimension_numbers=dims, preferred_element_type=jnp.float32)
    (lh, ll), (rh, rl) = left, right
    return dot(lh, rh) + (dot(lh, rl) + dot(ll, rh))


def orders(count):
    near = list(range(1, count))
    return near[GATHER_FROM:] + near[:GATHER_FROM], near[RESULT_FROM:] + near[:RESULT_FROM]


def paired(index, d, count):
    if d == 0:
        return index
    out, bit = 0, 1
    while bit < count:
        out = out + bit * ((index // bit + d // bit) % 2)
        bit *= 2
    return out


def factor(gram):
    side = gram.shape[0]
    rows = lax.broadcasted_iota(jnp.int32, (side, side), 0)
    cols = lax.broadcasted_iota(jnp.int32, (side, side), 1)
    eye = jnp.where(rows == cols, 1.0, 0.0).astype(jnp.float32)
    total = jnp.sum(jnp.sum(gram * eye, axis=1, keepdims=True), axis=0, keepdims=True)
    scale = lax.rsqrt(total + 1e-06)
    gram = gram * (scale * scale)
    held = None
    for step in range(ITERS):
        gs = split(gram)
        mixed = 3.4445 * eye - 4.775 * gram + 2.0315 * product(gs, gs, 0)
        ms = split(mixed)
        held = mixed if held is None else product(ms, split(held), 0)
        if step < ITERS - 1:
            gram = product(split(product(ms, gs, 0)), ms, 0)
    return held * scale


def kernel(nz, nw, chunks, per, grad, moment, weight, new_weights, new_momentum,
           grads, moments, weights, gather, grams, result, back,
           l_sem, w_sem, g_send, g_recv, p_send, p_recv, r_send, r_recv):
    zi, wi = lax.axis_index("zero"), lax.axis_index("width")
    mats = chunks * per
    rows, cols = grad.shape[1], grad.shape[2]
    side = nz * rows
    gather_order, result_order = orders(nz)
    pieces = [(d, k) for k in range(chunks) for d in gather_order + [0]]

    def partner(d):
        return paired(zi, d, nz)

    barrier = pltpu.get_barrier_semaphore()
    for d in range(1, nz):
        pl.semaphore_signal(barrier, inc=1, device_id={"zero": partner(d)}, device_id_type=MESH)
    for d in range(1, nw):
        pl.semaphore_signal(barrier, inc=1, device_id={"width": lax.rem(wi + d, nw)}, device_id_type=MESH)

    def piece(d, k):
        return pl.ds(partner(d) * mats + k * per, per)

    def load(which, d, k):
        source, target = ((grad, grads), (moment, moments))[which]
        return pltpu.make_async_copy(source.at[piece(d, k)], target.at[piece(d, k)], l_sem.at[which, d, k])

    def load_weight(k):
        part = pl.ds(k * nz * per, nz * per)
        return pltpu.make_async_copy(weight.at[part], weights.at[part], w_sem.at[k])

    def gather_copy(d, k):
        return pltpu.make_async_remote_copy(
            src_ref=new_momentum.at[piece(d, k)],
            dst_ref=gather.at[zi, pl.ds(k * per, per)],
            send_sem=g_send.at[d - 1, k], recv_sem=g_recv.at[d - 1, k],
            device_id={"zero": partner(d)}, device_id_type=MESH)

    def gram_copy(d, k):
        return pltpu.make_async_remote_copy(
            src_ref=grams.at[wi, pl.ds(k * per, per)],
            dst_ref=grams.at[wi, pl.ds(k * per, per)],
            send_sem=p_send.at[d - 1, k], recv_sem=p_recv.at[d - 1, k],
            device_id={"width": lax.rem(wi + d, nw)}, device_id_type=MESH)

    def result_copy(d, k):
        return pltpu.make_async_remote_copy(
            src_ref=result.at[partner(d), pl.ds(k * per, per)],
            dst_ref=back.at[piece(0, k)],
            send_sem=r_send.at[d - 1, k], recv_sem=r_recv.at[d - 1, k],
            device_id={"zero": partner(d)}, device_id_type=MESH)

    for d, k in pieces:
        load(0, d, k).start()
        load(1, d, k).start()

    def momentum(d, k):
        load(0, d, k).wait()
        load(1, d, k).wait()
        value = hold_rate * moments[piece(d, k)] + grads[piece(d, k)]
        new_momentum[piece(d, k)] = value
        if d == 0:
            gather[zi, pl.ds(k * per, per)] = value

    def release(d, k):
        if d:
            gather_copy(d, k).start()

    for n, (d, k) in enumerate(pieces):
        momentum(d, k)
        if n == 1:
            pl.semaphore_wait(barrier, nz + nw - 2)
        if n:
            release(*pieces[n - 1])
    release(*pieces[-1])
    for k in range(chunks):
        load_weight(k).start()

    def whole(i):
        return split(gather[:, i].reshape(side, cols))

    def finish(k):
        for d in range(1, nw):
            gram_copy(d, k).wait_recv()

        def one(j, carry):
            i = k * per + j
            gram = grams[0, i]
            for w in range(1, nw):
                gram = gram + grams[w, i]
            out = product(split(factor(gram)), whole(i), 0)
            result[:, i] = out.reshape(nz, rows, cols)
            return carry

        lax.fori_loop(0, per, one, 0)
        for d in result_order:
            result_copy(d, k).start()

    for k in range(chunks):
        for d in range(1, nz):
            gather_copy(d, k).wait_recv()

        def make(j, carry):
            i = k * per + j
            x = whole(i)
            grams[wi, i] = product(x, x, 1)
            return carry

        lax.fori_loop(0, per, make, 0)
        for d in range(1, nw):
            gram_copy(d, k).start()
        finish(k)

    for k in range(chunks):
        load_weight(k).wait()
    for k in range(chunks):
        new_weights[piece(0, k)] = keep_rate * weights[piece(0, k)] - learn_rate * result[zi, pl.ds(k * per, per)]
    for k in range(chunks):
        for d in result_order:
            result_copy(d, k).wait_recv()
            new_weights[piece(d, k)] = keep_rate * weights[piece(d, k)] - learn_rate * back[piece(d, k)]

    for k in range(chunks):
        for d in range(1, nz):
            gather_copy(d, k).wait_send()
            result_copy(d, k).wait_send()
        for d in range(1, nw):
            gram_copy(d, k).wait_send()


def by_kernel(nz, nw, grad, moment, weight):
    total, rows, cols = grad.shape
    side, mats = nz * rows, total // nz
    chunks = next(c for c in CHUNKS if mats % c == 0)
    dma = pltpu.SemaphoreType.DMA
    anywhere = pl.BlockSpec(memory_space=pl.ANY)
    shape = pltpu.VMEM(grad.shape, jnp.float32)
    local = pltpu.VMEM((total, rows, cols), jnp.float32)
    shared = pltpu.VMEM((nz, mats, rows, cols), jnp.float32)
    return pl.pallas_call(
        functools.partial(kernel, nz, nw, chunks, mats // chunks),
        out_shape=(shape, shape),
        in_specs=[anywhere] * 3,
        out_specs=(pl.BlockSpec(memory_space=pltpu.VMEM),) * 2,
        scratch_shapes=[
            local, local, local,
            shared,
            pltpu.VMEM((nw, mats, side, side), jnp.float32),
            shared,
            local,
            dma((2, nz, chunks)), dma((chunks,)),
            dma((nz - 1, chunks)), dma((nz - 1, chunks)),
            dma((nw - 1, chunks)), dma((nw - 1, chunks)),
            dma((nz - 1, chunks)), dma((nz - 1, chunks)),
        ],
        compiler_params=pltpu.CompilerParams(
            collective_id=0, has_side_effects=True, vmem_limit_bytes=40 * 2**20),
    )(*(pltpu.with_memory_space_constraint(x, pltpu.HBM) for x in (grad, moment, weight)))


def by_ops(new_momentum):
    moved = lax.all_to_all(new_momentum, "zero", split_axis=0, concat_axis=1, tiled=True)
    gram = jnp.einsum("mik,mjk->mij", moved, moved, precision=lax.Precision.HIGHEST)
    gram = lax.psum(gram, "width")
    eye = jnp.eye(gram.shape[1], dtype=jnp.float32)
    scale = lax.rsqrt(jnp.sum(gram * eye, axis=(1, 2), keepdims=True) + 1e-06)
    gram = gram * (scale * scale)
    dot = functools.partial(jnp.einsum, "mij,mjk->mik", precision=lax.Precision.HIGHEST)
    held = None
    for step in range(ITERS):
        mixed = 3.4445 * eye - 4.775 * gram + 2.0315 * dot(gram, gram)
        held = mixed if held is None else dot(mixed, held)
        gram = dot(dot(mixed, gram), mixed)
    out = dot(held * scale, moved)
    return lax.all_to_all(out, "zero", split_axis=1, concat_axis=0, tiled=True)


def body(nz, nw, grad_stack, moment_stack, weight_stack):
    if grad_stack.shape[1] % 8 == 0 and nz & (nz - 1) == 0:
        return by_kernel(nz, nw, grad_stack, moment_stack, weight_stack)
    new_momentum = hold_rate * moment_stack + grad_stack
    new_weights = keep_rate * weight_stack - learn_rate * by_ops(new_momentum)
    return (new_weights, new_momentum)


def solution(mesh):
    return jax.shard_map(
        functools.partial(body, mesh.shape["zero"], mesh.shape["width"]),
        mesh=mesh,
        in_specs=(
            P("unit", "zero", "width"),
            P("unit", "zero", "width"),
            P("unit", "zero", "width"),
        ),
        out_specs=(P("unit", "zero", "width"), P("unit", "zero", "width")),
        check_vma=False,
    )
```

profile of v0, /device:TPU:14, one launch (start us, length us, event | category | flops | bytes accessed | tf_op | source)
XLA Modules:
  0.0 97.9 jit_solution(5325031995159850811)
XLA Ops:
  0.6 94.6 %shard_map.50 = (f32[32,32,512]{2,1,0:T(8,128)S(1)}, f32[32,32,512]{2,1,0:T(8,128)S(1)}) custom-call(f32[32,32,512]{2,1,0:T(8,128)} %grad.1, f32[32,32,512]{2,1,0:T(8,128)} %moment.1, f32[32,32,512]{2,1,0:T(8,128)} %weight.1), custom_call_target="tpu_custom_call" | custom-call | tf_op jit(solution)/shard_map/pallas_call | solution.py:208
  95.2 1.3 %copy.7 = f32[32,32,512]{2,1,0:T(8,128)} copy(f32[32,32,512]{2,1,0:T(8,128)S(1)} %get-tuple-element.2) | data formatting | bytes 4194304
  96.5 1.3 %copy.8 = f32[32,32,512]{2,1,0:T(8,128)} copy(f32[32,32,512]{2,1,0:T(8,128)S(1)} %get-tuple-element.3) | data formatting | bytes 4194304
where the time goes:
time: 99.8 us; the launch traced here: 97.9 us
  Pallas kernels  94.6 us (95%)
  local copies, waits for them, and re-layouts  2.64 us (3%)
    pallas_call x1, Pallas kernels, by_kernel(): pl.pallas_call(functools.partial(kernel, nz, nw, chunks, mats // chunks),...  94.6 us
    unnamed x2, local copies, waits for them, and re-layouts  2.64 us

commit v1 on v0

--- a/solution.py
+++ b/solution.py
@@ -89,42 +89,50 @@
     def piece(d, k):
         return pl.ds(partner(d) * mats + k * per, per)
 
-    def load(which, d, k):
+    def group(n):
+        return 0 if n == 0 else 1 + n // nz
+
+    def load(which, n):
         source, target = ((grad, grads), (moment, moments))[which]
-        return pltpu.make_async_copy(source.at[piece(d, k)], target.at[piece(d, k)], l_sem.at[which, d, k])
-
-    def load_weight(k):
-        part = pl.ds(k * nz * per, nz * per)
-        return pltpu.make_async_copy(weight.at[part], weights.at[part], w_sem.at[k])
+        return pltpu.make_async_copy(source.at[piece(*pieces[n])], target.at[piece(*pieces[n])], l_sem.at[group(n)])
+
+    def load_weight():
+        return pltpu.make_async_copy(weight, weights, w_sem.at[0])
+
+    def wait_all(sem, *refs):
+        for ref in refs:
+            pltpu.make_async_copy(ref, ref, sem).wait()
 
     def gather_copy(d, k):
         return pltpu.make_async_remote_copy(
             src_ref=new_momentum.at[piece(d, k)],
             dst_ref=gather.at[zi, pl.ds(k * per, per)],
-            send_sem=g_send.at[d - 1, k], recv_sem=g_recv.at[d - 1, k],
+            send_sem=g_send.at[0], recv_sem=g_recv.at[k],
             device_id={"zero": partner(d)}, device_id_type=MESH)
 
     def gram_copy(d, k):
         return pltpu.make_async_remote_copy(
             src_ref=grams.at[wi, pl.ds(k * per, per)],
             dst_ref=grams.at[wi, pl.ds(k * per, per)],
-            send_sem=p_send.at[d - 1, k], recv_sem=p_recv.at[d - 1, k],
+            send_sem=p_send.at[0], recv_sem=p_recv.at[k],
             device_id={"width": lax.rem(wi + d, nw)}, device_id_type=MESH)
 
     def result_copy(d, k):
         return pltpu.make_async_remote_copy(
             src_ref=result.at[partner(d), pl.ds(k * per, per)],
             dst_ref=back.at[piece(0, k)],
-            send_sem=r_send.at[d - 1, k], recv_sem=r_recv.at[d - 1, k],
+            send_sem=r_send.at[0], recv_sem=r_recv.at[k],
             device_id={"zero": partner(d)}, device_id_type=MESH)
 
-    for d, k in pieces:
-        load(0, d, k).start()
-        load(1, d, k).start()
-
-    def momentum(d, k):
-        load(0, d, k).wait()
-        load(1, d, k).wait()
+    for n in range(len(pieces)):
+        load(0, n).start()
+        load(1, n).start()
+
+    def momentum(n):
+        d, k = pieces[n]
+        if n == 0 or group(n) != group(n - 1):
+            members = sum(group(m) == group(n) for m in range(len(pieces)))
+            wait_all(l_sem.at[group(n)], grads.at[pl.ds(0, 2 * members * per)])
         value = hold_rate * moments[piece(d, k)] + grads[piece(d, k)]
         new_momentum[piece(d, k)] = value
         if d == 0:
@@ -134,22 +142,20 @@
         if d:
             gather_copy(d, k).start()
 
-    for n, (d, k) in enumerate(pieces):
-        momentum(d, k)
+    for n in range(len(pieces)):
+        momentum(n)
         if n == 1:
             pl.semaphore_wait(barrier, nz + nw - 2)
         if n:
             release(*pieces[n - 1])
     release(*pieces[-1])
-    for k in range(chunks):
-        load_weight(k).start()
+    load_weight().start()
 
     def whole(i):
         return split(gather[:, i].reshape(side, cols))
 
     def finish(k):
-        for d in range(1, nw):
-            gram_copy(d, k).wait_recv()
+        wait_all(p_recv.at[k], grams.at[pl.ds(0, nw - 1), pl.ds(k * per, per)])
 
         def one(j, carry):
             i = k * per + j
@@ -165,8 +171,7 @@
             result_copy(d, k).start()
 
     for k in range(chunks):
-        for d in range(1, nz):
-            gather_copy(d, k).wait_recv()
+        wait_all(g_recv.at[k], gather.at[pl.ds(0, nz - 1), pl.ds(k * per, per)])
 
         def make(j, carry):
             i = k * per + j
@@ -179,21 +184,17 @@
             gram_copy(d, k).start()
         finish(k)
 
-    for k in range(chunks):
-        load_weight(k).wait()
+    load_weight().wait()
     for k in range(chunks):
         new_weights[piece(0, k)] = keep_rate * weights[piece(0, k)] - learn_rate * result[zi, pl.ds(k * per, per)]
     for k in range(chunks):
+        wait_all(r_recv.at[k], back.at[pl.ds(0, (nz - 1) * per)])
         for d in result_order:
-            result_copy(d, k).wait_recv()
             new_weights[piece(d, k)] = keep_rate * weights[piece(d, k)] - learn_rate * back[piece(d, k)]
 
-    for k in range(chunks):
-        for d in range(1, nz):
-            gather_copy(d, k).wait_send()
-            result_copy(d, k).wait_send()
-        for d in range(1, nw):
-            gram_copy(d, k).wait_send()
+    wait_all(g_send.at[0], gather.at[pl.ds(0, nz - 1)])
+    wait_all(p_send.at[0], grams.at[pl.ds(0, nw - 1)])
+    wait_all(r_send.at[0], result.at[pl.ds(0, nz - 1)])
 
 
 def by_kernel(nz, nw, grad, moment, weight):
@@ -216,10 +217,10 @@
             pltpu.VMEM((nw, mats, side, side), jnp.float32),
             shared,
             local,
-            dma((2, nz, chunks)), dma((chunks,)),
-            dma((nz - 1, chunks)), dma((nz - 1, chunks)),
-            dma((nw - 1, chunks)), dma((nw - 1, chunks)),
-            dma((nz - 1, chunks)), dma((nz - 1, chunks)),
+            dma((chunks + 1,)), dma((1,)),
+            dma((1,)), dma((chunks,)),
+            dma((1,)), dma((chunks,)),
+            dma((1,)), dma((chunks,)),
         ],
         compiler_params=pltpu.CompilerParams(
             collective_id=0, has_side_effects=True, vmem_limit_bytes=40 * 2**20),

time: 99.8 us -> 98.9 us (level)
  no operation moved by 1% of the time
where the time goes in v1:
time: 98.9 us; the launch traced here: 97.1 us
  Pallas kernels  93.9 us (95%)
  local copies, waits for them, and re-layouts  2.64 us (3%)
    pallas_call x1, Pallas kernels, by_kernel(): pl.pallas_call(functools.partial(kernel, nz, nw, chunks, mats // chunks),...  93.9 us
    unnamed x2, local copies, waits for them, and re-layouts  2.64 us

profile of v1, /device:TPU:14, one launch (start us, length us, event | category | flops | bytes accessed | tf_op | source)
XLA Modules:
  0.0 97.1 jit_solution(15291861906179526969)
XLA Ops:
  0.6 93.9 %shard_map.50 = (f32[32,32,512]{2,1,0:T(8,128)S(1)}, f32[32,32,512]{2,1,0:T(8,128)S(1)}) custom-call(f32[32,32,512]{2,1,0:T(8,128)} %grad.1, f32[32,32,512]{2,1,0:T(8,128)} %moment.1, f32[32,32,512]{2,1,0:T(8,128)} %weight.1), custom_call_target="tpu_custom_call" | custom-call | tf_op jit(solution)/shard_map/pallas_call | solution.py:209
  94.5 1.3 %copy.7 = f32[32,32,512]{2,1,0:T(8,128)} copy(f32[32,32,512]{2,1,0:T(8,128)S(1)} %get-tuple-element.2) | data formatting | bytes 4194304
  95.8 1.3 %copy.8 = f32[32,32,512]{2,1,0:T(8,128)} copy(f32[32,32,512]{2,1,0:T(8,128)S(1)} %get-tuple-element.3) | data formatting | bytes 4194304

commit v2 on v1

--- a/solution.py
+++ b/solution.py
@@ -11,6 +11,7 @@
 GATHER_FROM = 1
 RESULT_FROM = 1
 CHUNKS = (4, 2, 1)
+PARTS = (8, 4, 2, 1)
 MESH = pl.DeviceIdType.MESH
 
 
@@ -197,6 +198,31 @@
     wait_all(r_send.at[0], result.at[pl.ds(0, nz - 1)])
 
 
+def store(*refs):
+    count = len(refs) // 2
+    sem = refs[-1]
+    length = refs[0].shape[0]
+    parts = next(p for p in PARTS if length % p == 0)
+    for p in range(parts):
+        part = pl.ds(p * length // parts, length // parts)
+        for n in range(count):
+            pltpu.make_async_copy(refs[n].at[part], refs[count + n].at[part], sem.at[n]).start()
+    for n in range(count):
+        pltpu.make_async_copy(refs[n], refs[count + n], sem.at[n]).wait()
+
+
+def stored(*arrays):
+    inside = pl.BlockSpec(memory_space=pltpu.VMEM)
+    return pl.pallas_call(
+        store,
+        out_shape=tuple(pltpu.HBM(x.shape, x.dtype) for x in arrays),
+        in_specs=[inside] * len(arrays),
+        out_specs=(pl.BlockSpec(memory_space=pltpu.HBM),) * len(arrays),
+        scratch_shapes=[pltpu.SemaphoreType.DMA((len(arrays),))],
+        compiler_params=pltpu.CompilerParams(vmem_limit_bytes=2**20),
+    )(*(pltpu.with_memory_space_constraint(x, pltpu.VMEM) for x in arrays))
+
+
 def by_kernel(nz, nw, grad, moment, weight):
     total, rows, cols = grad.shape
     side, mats = nz * rows, total // nz
@@ -206,7 +232,7 @@
     shape = pltpu.VMEM(grad.shape, jnp.float32)
     local = pltpu.VMEM((total, rows, cols), jnp.float32)
     shared = pltpu.VMEM((nz, mats, rows, cols), jnp.float32)
-    return pl.pallas_call(
+    results = pl.pallas_call(
         functools.partial(kernel, nz, nw, chunks, mats // chunks),
         out_shape=(shape, shape),
         in_specs=[anywhere] * 3,
@@ -225,6 +251,7 @@
         compiler_params=pltpu.CompilerParams(
             collective_id=0, has_side_effects=True, vmem_limit_bytes=40 * 2**20),
     )(*(pltpu.with_memory_space_constraint(x, pltpu.HBM) for x in (grad, moment, weight)))
+    return stored(*results)
 
 
 def by_ops(new_momentum):

time: 98.9 us -> 98.3 us (level)
  local copies, waits for them, and re-layouts: 2.64 us -> 0 us
  Pallas kernels: 93.9 us -> 95.9 us
    unnamed x2 -> x0, local copies, waits for them, and re-layouts: 2.64 us -> none
    pallas_call x0 -> x1, Pallas kernels: none -> 2.01 us  [stored(): pl.pallas_call(store, out_shape=tuple((pltpu.HBM(x.shape, x.dtype) for x...]
where the time goes in v2:
time: 98.3 us; the launch traced here: 96.5 us
  Pallas kernels  95.9 us (98%)
    pallas_call x1, Pallas kernels, by_kernel(): pl.pallas_call(functools.partial(kernel, nz, nw, chunks, mats // chunks),...  93.9 us
    pallas_call x1, Pallas kernels, stored(): pl.pallas_call(store, out_shape=tuple((pltpu.HBM(x.shape, x.dtype) for x...  2.01 us

profile of v2, /device:TPU:14, one launch (start us, length us, event | category | flops | bytes accessed | tf_op | source)
XLA Modules:
  0.0 96.5 jit_solution(18182350365346294848)
XLA Ops:
  0.6 93.9 %shard_map.50 = (f32[32,32,512]{2,1,0:T(8,128)S(1)}, f32[32,32,512]{2,1,0:T(8,128)S(1)}) custom-call(f32[32,32,512]{2,1,0:T(8,128)} %grad.1, f32[32,32,512]{2,1,0:T(8,128)} %moment.1, f32[32,32,512]{2,1,0:T(8,128)} %weight.1), custom_call_target="tpu_custom_call" | custom-call | tf_op jit(solution)/shard_map/pallas_call | solution.py:235
  94.5 2.0 %shard_map.51 = (f32[32,32,512]{2,1,0:T(8,128)}, f32[32,32,512]{2,1,0:T(8,128)}) custom-call(f32[32,32,512]{2,1,0:T(8,128)S(1)} %get-tuple-element.4.refs_0_, f32[32,32,512]{2,1,0:T(8,128)S(1)} %get-tuple-element.5.refs_1_), custom_call_target="tpu_custom_call" | custom-call | tf_op jit(solution)/shard_map/pallas_call | solution.py:216

commit v3 on v2

--- a/solution.py
+++ b/solution.py
@@ -12,6 +12,7 @@
 RESULT_FROM = 1
 CHUNKS = (4, 2, 1)
 PARTS = (8, 4, 2, 1)
+AHEAD = 2
 MESH = pl.DeviceIdType.MESH
 
 
@@ -70,22 +71,44 @@
 
 def kernel(nz, nw, chunks, per, grad, moment, weight, new_weights, new_momentum,
            grads, moments, weights, gather, grams, result, back,
-           l_sem, w_sem, g_send, g_recv, p_send, p_recv, r_send, r_recv):
+           l_sem, w_sem, g_send, g_recv, p_send, p_recv, r_send, r_recv, column, all_in):
     zi, wi = lax.axis_index("zero"), lax.axis_index("width")
     mats = chunks * per
     rows, cols = grad.shape[1], grad.shape[2]
     side = nz * rows
     gather_order, result_order = orders(nz)
-    pieces = [(d, k) for k in range(chunks) for d in gather_order + [0]]
+    ahead = min(AHEAD, chunks)
+    far = nz - 1
+    pieces = [(far, k) for k in range(ahead)]
+    pieces += [(d, k) for k in range(ahead) for d in gather_order if d != far]
+    pieces += [(d, k) for k in range(ahead, chunks) for d in gather_order]
+    pieces += [(0, k) for k in range(chunks)]
+    inners = (nz // 2 - 1, nz // 2)
+    outers = [z for z in range(nz) if z not in inners]
+    inner = (zi == inners[0]) | (zi == inners[1])
+    outer = jnp.logical_not(inner)
 
     def partner(d):
         return paired(zi, d, nz)
 
     barrier = pltpu.get_barrier_semaphore()
-    for d in range(1, nz):
-        pl.semaphore_signal(barrier, inc=1, device_id={"zero": partner(d)}, device_id_type=MESH)
-    for d in range(1, nw):
-        pl.semaphore_signal(barrier, inc=1, device_id={"width": lax.rem(wi + d, nw)}, device_id_type=MESH)
+
+    def tell(sem, axis, index):
+        pl.semaphore_signal(sem, inc=1, device_id={axis: index}, device_id_type=MESH)
+
+    @pl.when(inner)
+    def _():
+        tell(barrier, "zero", partner(far))
+
+    for z in outers:
+        @pl.when(zi != z)
+        def _():
+            tell(barrier, "zero", z)
+
+    @pl.when(outer)
+    def _():
+        for d in range(1, nw):
+            tell(barrier, "width", lax.rem(wi + d, nw))
 
     def piece(d, k):
         return pl.ds(partner(d) * mats + k * per, per)
@@ -146,11 +169,28 @@
     for n in range(len(pieces)):
         momentum(n)
         if n == 1:
-            pl.semaphore_wait(barrier, nz + nw - 2)
+            pl.semaphore_wait(barrier, jnp.where(inner, 1, nz + nw - 2))
+
+            @pl.when(outer)
+            def _():
+                for z in inners:
+                    tell(column, "zero", z)
+                for d in range(1, nw):
+                    tell(all_in, "width", lax.rem(wi + d, nw))
+        if n == ahead + 1:
+            @pl.when(inner)
+            def _():
+                pl.semaphore_wait(column, len(outers))
         if n:
             release(*pieces[n - 1])
     release(*pieces[-1])
     load_weight().start()
+
+    @pl.when(outer)
+    def _():
+        pl.semaphore_wait(all_in, nw - 1)
+        for z in inners:
+            tell(all_in, "zero", z)
 
     def whole(i):
         return split(gather[:, i].reshape(side, cols))
@@ -181,6 +221,10 @@
             return carry
 
         lax.fori_loop(0, per, make, 0)
+        if k == 0:
+            @pl.when(inner)
+            def _():
+                pl.semaphore_wait(all_in, len(outers))
         for d in range(1, nw):
             gram_copy(d, k).start()
         finish(k)
@@ -247,6 +291,7 @@
             dma((1,)), dma((chunks,)),
             dma((1,)), dma((chunks,)),
             dma((1,)), dma((chunks,)),
+            pltpu.SemaphoreType.REGULAR, pltpu.SemaphoreType.REGULAR,
         ],
         compiler_params=pltpu.CompilerParams(
             collective_id=0, has_side_effects=True, vmem_limit_bytes=40 * 2**20),
@@ -272,7 +317,7 @@
 
 
 def body(nz, nw, grad_stack, moment_stack, weight_stack):
-    if grad_stack.shape[1] % 8 == 0 and nz & (nz - 1) == 0:
+    if grad_stack.shape[1] % 8 == 0 and nz & (nz - 1) == 0 and nz > 2:
         return by_kernel(nz, nw, grad_stack, moment_stack, weight_stack)
     new_momentum = hold_rate * moment_stack + grad_stack
     new_weights = keep_rate * weight_stack - learn_rate * by_ops(new_momentum)

time: 98.3 us -> 97.2 us (0.989); the launches traced: 96.5 us -> 96.6 us
  no operation moved by 1% of the time
where the time goes in v3:
time: 97.2 us; the launch traced here: 96.6 us
  Pallas kernels  95.9 us (99%)
    pallas_call x1, Pallas kernels, by_kernel(): pl.pallas_call(functools.partial(kernel, nz, nw, chunks, mats // chunks),...  93.9 us
    pallas_call x1, Pallas kernels, stored(): pl.pallas_call(store, out_shape=tuple((pltpu.HBM(x.shape, x.dtype) for x...  2.01 us

profile of v3, /device:TPU:14, one launch (start us, length us, event | category | flops | bytes accessed | tf_op | source)
XLA Modules:
  0.0 96.6 jit_solution(3976842049872347086)
XLA Ops:
  0.6 93.9 %shard_map.50 = (f32[32,32,512]{2,1,0:T(8,128)S(1)}, f32[32,32,512]{2,1,0:T(8,128)S(1)}) custom-call(f32[32,32,512]{2,1,0:T(8,128)} %grad.1, f32[32,32,512]{2,1,0:T(8,128)} %moment.1, f32[32,32,512]{2,1,0:T(8,128)} %weight.1), custom_call_target="tpu_custom_call" | custom-call | tf_op jit(solution)/shard_map/pallas_call | solution.py:279
  94.6 2.0 %shard_map.51 = (f32[32,32,512]{2,1,0:T(8,128)}, f32[32,32,512]{2,1,0:T(8,128)}) custom-call(f32[32,32,512]{2,1,0:T(8,128)S(1)} %get-tuple-element.4.refs_0_, f32[32,32,512]{2,1,0:T(8,128)S(1)} %get-tuple-element.5.refs_1_), custom_call_target="tpu_custom_call" | custom-call | tf_op jit(solution)/shard_map/pallas_call | solution.py:260

commit v4 on v3

--- a/solution.py
+++ b/solution.py
@@ -96,20 +96,6 @@
     def tell(sem, axis, index):
         pl.semaphore_signal(sem, inc=1, device_id={axis: index}, device_id_type=MESH)
 
-    @pl.when(inner)
-    def _():
-        tell(barrier, "zero", partner(far))
-
-    for z in outers:
-        @pl.when(zi != z)
-        def _():
-            tell(barrier, "zero", z)
-
-    @pl.when(outer)
-    def _():
-        for d in range(1, nw):
-            tell(barrier, "width", lax.rem(wi + d, nw))
-
     def piece(d, k):
         return pl.ds(partner(d) * mats + k * per, per)
 
@@ -148,7 +134,23 @@
             send_sem=r_send.at[0], recv_sem=r_recv.at[k],
             device_id={"zero": partner(d)}, device_id_type=MESH)
 
-    for n in range(len(pieces)):
+    @pl.when(inner)
+    def _():
+        tell(barrier, "zero", partner(far))
+
+    load(0, 0).start()
+    load(1, 0).start()
+    for z in outers:
+        @pl.when(zi != z)
+        def _():
+            tell(barrier, "zero", z)
+
+    @pl.when(outer)
+    def _():
+        for d in range(1, nw):
+            tell(barrier, "width", lax.rem(wi + d, nw))
+
+    for n in range(1, len(pieces)):
         load(0, n).start()
         load(1, n).start()
 
@@ -168,8 +170,9 @@
 
     for n in range(len(pieces)):
         momentum(n)
-        if n == 1:
+        if n == 0:
             pl.semaphore_wait(barrier, jnp.where(inner, 1, nz + nw - 2))
+            release(*pieces[0])
 
             @pl.when(outer)
             def _():
@@ -181,7 +184,7 @@
             @pl.when(inner)
             def _():
                 pl.semaphore_wait(column, len(outers))
-        if n:
+        if n > 1:
             release(*pieces[n - 1])
     release(*pieces[-1])
     load_weight().start()
@@ -208,8 +211,13 @@
             return carry
 
         lax.fori_loop(0, per, one, 0)
-        for d in result_order:
-            result_copy(d, k).start()
+        results = [(d, k) for d in result_order if d != far]
+        if k > 0:
+            results.insert(1, (far, k - 1))
+        if k == chunks - 1:
+            results.append((far, k))
+        for piece_of in results:
+            result_copy(*piece_of).start()
 
     for k in range(chunks):
         wait_all(g_recv.at[k], gather.at[pl.ds(0, nz - 1), pl.ds(k * per, per)])

time: 97.2 us -> 96.5 us (level)
  no operation moved by 1% of the time
where the time goes in v4:
time: 96.5 us; the launch traced here: 96.2 us
  Pallas kernels  95.6 us (99%)
    pallas_call x1, Pallas kernels, by_kernel(): pl.pallas_call(functools.partial(kernel, nz, nw, chunks, mats // chunks),...  93.6 us
    pallas_call x1, Pallas kernels, stored(): pl.pallas_call(store, out_shape=tuple((pltpu.HBM(x.shape, x.dtype) for x...  2.01 us

profile of v4, /device:TPU:14, one launch (start us, length us, event | category | flops | bytes accessed | tf_op | source)
XLA Modules:
  0.0 96.2 jit_solution(14736618684408482495)
XLA Ops:
  0.6 93.6 %shard_map.50 = (f32[32,32,512]{2,1,0:T(8,128)S(1)}, f32[32,32,512]{2,1,0:T(8,128)S(1)}) custom-call(f32[32,32,512]{2,1,0:T(8,128)} %grad.1, f32[32,32,512]{2,1,0:T(8,128)} %moment.1, f32[32,32,512]{2,1,0:T(8,128)} %weight.1), custom_call_target="tpu_custom_call" | custom-call | tf_op jit(solution)/shard_map/pallas_call | solution.py:287
  94.2 2.0 %shard_map.51 = (f32[32,32,512]{2,1,0:T(8,128)}, f32[32,32,512]{2,1,0:T(8,128)}) custom-call(f32[32,32,512]{2,1,0:T(8,128)S(1)} %get-tuple-element.4.refs_0_, f32[32,32,512]{2,1,0:T(8,128)S(1)} %get-tuple-element.5.refs_1_), custom_call_target="tpu_custom_call" | custom-call | tf_op jit(solution)/shard_map/pallas_call | solution.py:268

commit v5 on v4

--- a/solution.py
+++ b/solution.py
@@ -11,7 +11,7 @@
 GATHER_FROM = 1
 RESULT_FROM = 1
 CHUNKS = (4, 2, 1)
-PARTS = (8, 4, 2, 1)
+PARTS = (16, 8, 4, 2, 1)
 AHEAD = 2
 MESH = pl.DeviceIdType.MESH
 
@@ -100,7 +100,7 @@
         return pl.ds(partner(d) * mats + k * per, per)
 
     def group(n):
-        return 0 if n == 0 else 1 + n // nz
+        return 0 if n == 0 else 1 + 2 * n // len(pieces)
 
     def load(which, n):
         source, target = ((grad, grads), (moment, moments))[which]
@@ -131,15 +131,18 @@
         return pltpu.make_async_remote_copy(
             src_ref=result.at[partner(d), pl.ds(k * per, per)],
             dst_ref=back.at[piece(0, k)],
-            send_sem=r_send.at[0], recv_sem=r_recv.at[k],
+            send_sem=r_send.at[0], recv_sem=r_recv.at[int(k == chunks - 1)],
             device_id={"zero": partner(d)}, device_id_type=MESH)
 
     @pl.when(inner)
     def _():
         tell(barrier, "zero", partner(far))
 
-    load(0, 0).start()
-    load(1, 0).start()
+    for i in range(per):
+        for row in range(0, rows, 8):
+            for source, target in ((grad, grads), (moment, moments)):
+                part = (partner(far) * mats + i, pl.ds(row, 8))
+                pltpu.make_async_copy(source.at[part], target.at[part], l_sem.at[0]).start()
     for z in outers:
         @pl.when(zi != z)
         def _():
@@ -219,7 +222,7 @@
         for piece_of in results:
             result_copy(*piece_of).start()
 
-    for k in range(chunks):
+    def begin(k):
         wait_all(g_recv.at[k], gather.at[pl.ds(0, nz - 1), pl.ds(k * per, per)])
 
         def make(j, carry):
@@ -235,18 +238,27 @@
                 pl.semaphore_wait(all_in, len(outers))
         for d in range(1, nw):
             gram_copy(d, k).start()
+
+    for k in range(ahead):
+        begin(k)
+    for k in range(ahead):
+        finish(k)
+    for k in range(ahead, chunks):
+        begin(k)
         finish(k)
 
     load_weight().wait()
     for k in range(chunks):
         new_weights[piece(0, k)] = keep_rate * weights[piece(0, k)] - learn_rate * result[zi, pl.ds(k * per, per)]
-    for k in range(chunks):
-        wait_all(r_recv.at[k], back.at[pl.ds(0, (nz - 1) * per)])
-        for d in result_order:
-            new_weights[piece(d, k)] = keep_rate * weights[piece(d, k)] - learn_rate * back[piece(d, k)]
-
     wait_all(g_send.at[0], gather.at[pl.ds(0, nz - 1)])
     wait_all(p_send.at[0], grams.at[pl.ds(0, nw - 1)])
+    for part, members in enumerate((range(chunks - 1), range(chunks - 1, chunks))):
+        if members:
+            wait_all(r_recv.at[part], back.at[pl.ds(0, (nz - 1) * per * len(members))])
+        for k in members:
+            for d in result_order:
+                new_weights[piece(d, k)] = keep_rate * weights[piece(d, k)] - learn_rate * back[piece(d, k)]
+
     wait_all(r_send.at[0], result.at[pl.ds(0, nz - 1)])
 
 
@@ -295,10 +307,10 @@
             pltpu.VMEM((nw, mats, side, side), jnp.float32),
             shared,
             local,
-            dma((chunks + 1,)), dma((1,)),
+            dma((3,)), dma((1,)),
             dma((1,)), dma((chunks,)),
             dma((1,)), dma((chunks,)),
-            dma((1,)), dma((chunks,)),
+            dma((1,)), dma((2,)),
             pltpu.SemaphoreType.REGULAR, pltpu.SemaphoreType.REGULAR,
         ],
         compiler_params=pltpu.CompilerParams(

time: 96.5 us -> 96.3 us (level)
  no operation moved by 1% of the time
where the time goes in v5:
time: 96.3 us; the launch traced here: 96.1 us
  Pallas kernels  95.5 us (99%)
    pallas_call x1, Pallas kernels, by_kernel(): pl.pallas_call(functools.partial(kernel, nz, nw, chunks, mats // chunks),...  93.5 us
    pallas_call x1, Pallas kernels, stored(): pl.pallas_call(store, out_shape=tuple((pltpu.HBM(x.shape, x.dtype) for x...  2 us

profile of v5, /device:TPU:14, one launch (start us, length us, event | category | flops | bytes accessed | tf_op | source)
XLA Modules:
  0.0 96.1 jit_solution(9261189396481152027)
XLA Ops:
  0.6 93.5 %shard_map.50 = (f32[32,32,512]{2,1,0:T(8,128)S(1)}, f32[32,32,512]{2,1,0:T(8,128)S(1)}) custom-call(f32[32,32,512]{2,1,0:T(8,128)} %grad.1, f32[32,32,512]{2,1,0:T(8,128)} %moment.1, f32[32,32,512]{2,1,0:T(8,128)} %weight.1), custom_call_target="tpu_custom_call" | custom-call | tf_op jit(solution)/shard_map/pallas_call | solution.py:299
  94.1 2.0 %shard_map.51 = (f32[32,32,512]{2,1,0:T(8,128)}, f32[32,32,512]{2,1,0:T(8,128)}) custom-call(f32[32,32,512]{2,1,0:T(8,128)S(1)} %get-tuple-element.4.refs_0_, f32[32,32,512]{2,1,0:T(8,128)S(1)} %get-tuple-element.5.refs_1_), custom_call_target="tpu_custom_call" | custom-call | tf_op jit(solution)/shard_map/pallas_call | solution.py:280

commit v6 on v5

--- a/solution.py
+++ b/solution.py
@@ -11,8 +11,9 @@
 GATHER_FROM = 1
 RESULT_FROM = 1
 CHUNKS = (4, 2, 1)
-PARTS = (16, 8, 4, 2, 1)
-AHEAD = 2
+PARTS = (32, 16, 8, 4, 2, 1)
+AHEAD = 3
+PLAN = 2
 MESH = pl.DeviceIdType.MESH
 
 
@@ -71,7 +72,7 @@
 
 def kernel(nz, nw, chunks, per, grad, moment, weight, new_weights, new_momentum,
            grads, moments, weights, gather, grams, result, back,
-           l_sem, w_sem, g_send, g_recv, p_send, p_recv, r_send, r_recv, column, all_in):
+           l_sem, g_send, g_recv, p_recv, r_recv, column, all_in):
     zi, wi = lax.axis_index("zero"), lax.axis_index("width")
     mats = chunks * per
     rows, cols = grad.shape[1], grad.shape[2]
@@ -107,7 +108,7 @@
         return pltpu.make_async_copy(source.at[piece(*pieces[n])], target.at[piece(*pieces[n])], l_sem.at[group(n)])
 
     def load_weight():
-        return pltpu.make_async_copy(weight, weights, w_sem.at[0])
+        return pltpu.make_async_copy(weight, weights, l_sem.at[0])
 
     def wait_all(sem, *refs):
         for ref in refs:
@@ -124,14 +125,14 @@
         return pltpu.make_async_remote_copy(
             src_ref=grams.at[wi, pl.ds(k * per, per)],
             dst_ref=grams.at[wi, pl.ds(k * per, per)],
-            send_sem=p_send.at[0], recv_sem=p_recv.at[k],
+            send_sem=l_sem.at[1], recv_sem=p_recv.at[k],
             device_id={"width": lax.rem(wi + d, nw)}, device_id_type=MESH)
 
     def result_copy(d, k):
         return pltpu.make_async_remote_copy(
             src_ref=result.at[partner(d), pl.ds(k * per, per)],
             dst_ref=back.at[piece(0, k)],
-            send_sem=r_send.at[0], recv_sem=r_recv.at[int(k == chunks - 1)],
+            send_sem=l_sem.at[2], recv_sem=r_recv.at[int(k == chunks - 1)],
             device_id={"zero": partner(d)}, device_id_type=MESH)
 
     @pl.when(inner)
@@ -239,11 +240,11 @@
         for d in range(1, nw):
             gram_copy(d, k).start()
 
-    for k in range(ahead):
+    for k in range(min(PLAN, chunks)):
         begin(k)
-    for k in range(ahead):
+    for k in range(min(PLAN, chunks)):
         finish(k)
-    for k in range(ahead, chunks):
+    for k in range(min(PLAN, chunks), chunks):
         begin(k)
         finish(k)
 
@@ -251,7 +252,7 @@
     for k in range(chunks):
         new_weights[piece(0, k)] = keep_rate * weights[piece(0, k)] - learn_rate * result[zi, pl.ds(k * per, per)]
     wait_all(g_send.at[0], gather.at[pl.ds(0, nz - 1)])
-    wait_all(p_send.at[0], grams.at[pl.ds(0, nw - 1)])
+    wait_all(l_sem.at[1], grams.at[pl.ds(0, nw - 1)])
     for part, members in enumerate((range(chunks - 1), range(chunks - 1, chunks))):
         if members:
             wait_all(r_recv.at[part], back.at[pl.ds(0, (nz - 1) * per * len(members))])
@@ -259,7 +260,7 @@
             for d in result_order:
                 new_weights[piece(d, k)] = keep_rate * weights[piece(d, k)] - learn_rate * back[piece(d, k)]
 
-    wait_all(r_send.at[0], result.at[pl.ds(0, nz - 1)])
+    wait_all(l_sem.at[2], result.at[pl.ds(0, nz - 1)])
 
 
 def store(*refs):
@@ -307,10 +308,9 @@
             pltpu.VMEM((nw, mats, side, side), jnp.float32),
             shared,
             local,
-            dma((3,)), dma((1,)),
+            dma((3,)),
             dma((1,)), dma((chunks,)),
-            dma((1,)), dma((chunks,)),
-            dma((1,)), dma((2,)),
+            dma((chunks,)), dma((2,)),
             pltpu.SemaphoreType.REGULAR, pltpu.SemaphoreType.REGULAR,
         ],
         compiler_params=pltpu.CompilerParams(

time: 96.3 us -> 96.2 us (level)
  no operation moved by 1% of the time
where the time goes in v6:
time: 96.2 us; the launch traced here: 96 us
  Pallas kernels  95.4 us (99%)
    pallas_call x1, Pallas kernels, by_kernel(): pl.pallas_call(functools.partial(kernel, nz, nw, chunks, mats // chunks),...  93.4 us
    pallas_call x1, Pallas kernels, stored(): pl.pallas_call(store, out_shape=tuple((pltpu.HBM(x.shape, x.dtype) for x...  1.98 us

profile of v6, /device:TPU:14, one launch (start us, length us, event | category | flops | bytes accessed | tf_op | source)
XLA Modules:
  0.0 96.0 jit_solution(15331381575367323256)
XLA Ops:
  0.6 93.4 %shard_map.50 = (f32[32,32,512]{2,1,0:T(8,128)S(1)}, f32[32,32,512]{2,1,0:T(8,128)S(1)}) custom-call(f32[32,32,512]{2,1,0:T(8,128)} %grad.1, f32[32,32,512]{2,1,0:T(8,128)} %moment.1, f32[32,32,512]{2,1,0:T(8,128)} %weight.1), custom_call_target="tpu_custom_call" | custom-call | tf_op jit(solution)/shard_map/pallas_call | solution.py:300
  94.0 2.0 %shard_map.51 = (f32[32,32,512]{2,1,0:T(8,128)}, f32[32,32,512]{2,1,0:T(8,128)}) custom-call(f32[32,32,512]{2,1,0:T(8,128)S(1)} %get-tuple-element.4.refs_0_, f32[32,32,512]{2,1,0:T(8,128)S(1)} %get-tuple-element.5.refs_1_), custom_call_target="tpu_custom_call" | custom-call | tf_op jit(solution)/shard_map/pallas_call | solution.py:281

commit v7 on v6

--- a/solution.py
+++ b/solution.py
@@ -132,7 +132,7 @@
         return pltpu.make_async_remote_copy(
             src_ref=result.at[partner(d), pl.ds(k * per, per)],
             dst_ref=back.at[piece(0, k)],
-            send_sem=l_sem.at[2], recv_sem=r_recv.at[int(k == chunks - 1)],
+            send_sem=l_sem.at[2], recv_sem=r_recv.at[(1 + int(d == far)) * int(k == chunks - 1)],
             device_id={"zero": partner(d)}, device_id_type=MESH)
 
     @pl.when(inner)
@@ -253,12 +253,13 @@
         new_weights[piece(0, k)] = keep_rate * weights[piece(0, k)] - learn_rate * result[zi, pl.ds(k * per, per)]
     wait_all(g_send.at[0], gather.at[pl.ds(0, nz - 1)])
     wait_all(l_sem.at[1], grams.at[pl.ds(0, nw - 1)])
-    for part, members in enumerate((range(chunks - 1), range(chunks - 1, chunks))):
+    last = chunks - 1
+    batches = [[(d, k) for k in range(last) for d in result_order], [(d, last) for d in result_order if d != far], [(far, last)]]
+    for part, members in enumerate(batches):
         if members:
-            wait_all(r_recv.at[part], back.at[pl.ds(0, (nz - 1) * per * len(members))])
-        for k in members:
-            for d in result_order:
-                new_weights[piece(d, k)] = keep_rate * weights[piece(d, k)] - learn_rate * back[piece(d, k)]
+            wait_all(r_recv.at[part], back.at[pl.ds(0, per * len(members))])
+        for d, k in members:
+            new_weights[piece(d, k)] = keep_rate * weights[piece(d, k)] - learn_rate * back[piece(d, k)]
 
     wait_all(l_sem.at[2], result.at[pl.ds(0, nz - 1)])
 
@@ -310,7 +311,7 @@
             local,
             dma((3,)),
             dma((1,)), dma((chunks,)),
-            dma((chunks,)), dma((2,)),
+            dma((chunks,)), dma((3,)),
             pltpu.SemaphoreType.REGULAR, pltpu.SemaphoreType.REGULAR,
         ],
         compiler_params=pltpu.CompilerParams(

time: 96.2 us -> 96.1 us (level)
  no operation moved by 1% of the time
where the time goes in v7:
time: 96.1 us; the launch traced here: 96 us
  Pallas kernels  95.3 us (99%)
    pallas_call x1, Pallas kernels, by_kernel(): pl.pallas_call(functools.partial(kernel, nz, nw, chunks, mats // chunks),...  93.4 us
    pallas_call x1, Pallas kernels, stored(): pl.pallas_call(store, out_shape=tuple((pltpu.HBM(x.shape, x.dtype) for x...  1.98 us

profile of v7, /device:TPU:14, one launch (start us, length us, event | category | flops | bytes accessed | tf_op | source)
XLA Modules:
  0.0 96.0 jit_solution(10880766825762838897)
XLA Ops:
  0.6 93.4 %shard_map.50 = (f32[32,32,512]{2,1,0:T(8,128)S(1)}, f32[32,32,512]{2,1,0:T(8,128)S(1)}) custom-call(f32[32,32,512]{2,1,0:T(8,128)} %grad.1, f32[32,32,512]{2,1,0:T(8,128)} %moment.1, f32[32,32,512]{2,1,0:T(8,128)} %weight.1), custom_call_target="tpu_custom_call" | custom-call | tf_op jit(solution)/shard_map/pallas_call | solution.py:301
  94.0 2.0 %shard_map.51 = (f32[32,32,512]{2,1,0:T(8,128)}, f32[32,32,512]{2,1,0:T(8,128)}) custom-call(f32[32,32,512]{2,1,0:T(8,128)S(1)} %get-tuple-element.4.refs_0_, f32[32,32,512]{2,1,0:T(8,128)S(1)} %get-tuple-element.5.refs_1_), custom_call_target="tpu_custom_call" | custom-call | tf_op jit(solution)/shard_map/pallas_call | solution.py:282

commit v8 on v7

--- a/solution.py
+++ b/solution.py
@@ -12,7 +12,7 @@
 RESULT_FROM = 1
 CHUNKS = (4, 2, 1)
 PARTS = (32, 16, 8, 4, 2, 1)
-AHEAD = 3
+AHEAD = 4
 PLAN = 2
 MESH = pl.DeviceIdType.MESH
 

time: 96.1 us -> 96.1 us (level)
  no operation moved by 1% of the time
where the time goes in v8:
time: 96.1 us; the launch traced here: 96 us
  Pallas kernels  95.3 us (99%)
    pallas_call x1, Pallas kernels, by_kernel(): pl.pallas_call(functools.partial(kernel, nz, nw, chunks, mats // chunks),...  93.4 us
    pallas_call x1, Pallas kernels, stored(): pl.pallas_call(store, out_shape=tuple((pltpu.HBM(x.shape, x.dtype) for x...  1.98 us

profile of v8, /device:TPU:14, one launch (start us, length us, event | category | flops | bytes accessed | tf_op | source)
XLA Modules:
  0.0 96.0 jit_solution(8965953921165762794)
XLA Ops:
  0.6 93.4 %shard_map.50 = (f32[32,32,512]{2,1,0:T(8,128)S(1)}, f32[32,32,512]{2,1,0:T(8,128)S(1)}) custom-call(f32[32,32,512]{2,1,0:T(8,128)} %grad.1, f32[32,32,512]{2,1,0:T(8,128)} %moment.1, f32[32,32,512]{2,1,0:T(8,128)} %weight.1), custom_call_target="tpu_custom_call" | custom-call | tf_op jit(solution)/shard_map/pallas_call | solution.py:301
  94.0 2.0 %shard_map.51 = (f32[32,32,512]{2,1,0:T(8,128)}, f32[32,32,512]{2,1,0:T(8,128)}) custom-call(f32[32,32,512]{2,1,0:T(8,128)S(1)} %get-tuple-element.4.refs_0_, f32[32,32,512]{2,1,0:T(8,128)S(1)} %get-tuple-element.5.refs_1_), custom_call_target="tpu_custom_call" | custom-call | tf_op jit(solution)/shard_map/pallas_call | solution.py:282
